TPU v7x, 32 devices: a whole 2x2x4 slice. The times are simulated.
32 devices in a mesh: group: 4 (over y, x), dp: 8 (over z, core).
Axes of the slice: x: 2, y: 2, z: 4, core: 2. Of those that a mesh axis runs over, the one named last changes fastest.
Arguments:
- observations: bfloat16 [64, 64, 4096], P('dp', None, 'group'), may hold values from -6 to 6
- next_observations: bfloat16 [1024, 4096], P('dp', 'group'), may hold values from -6 to 6
- trunk_weights: bfloat16 [2, 4096, 4096], P(None, 'dp', 'group'), may hold values from -0.125 to 0.125
- head_weights: bfloat16 [4096, 19], P('group'), may hold values from -0.25 to 0.25
- acting_policy_logits: float32 [64, 63, 18], P('dp'), may hold values from -16 to 330, as said below
- actions: int32 [64, 63], P('dp'), may hold values from 0 to 17
- rewards: float32 [64, 63], P('dp'), may hold values from -6 to 6
- episode_finished: int32 [64, 63], P('dp'), may hold values 0 or 1
Outputs:
- trunk_grads: float32 [2, 4096, 4096], P(None, 'dp', 'group')
- head_grads: float32 [4096, 19], P(('group', 'dp'))
- actor_logits: float32 [1024, 18], P('dp')
Inputs may be any that keep to these rules, and one draw needn't show every extreme that they name: `acting_policy_logits`: Real-valued scores, one row for each step and trajectory.
All inputs are finite; a program needn't handle non-finite values. No bound on the sum of `episode_finished` on one device may be relied on, other than what follows from the above.
Results may differ from a plain program's by a relative error of at most 0.012.
Values may be sent and summed in bfloat16 or wider, within the bound.
A program may use at most 128 MiB of HBM per device.

v0:
```python
import jax
import jax.numpy as jnp
from jax import lax
from jax.sharding import PartitionSpec as P

discount_rate = 0.99
value_weight = 0.5
entropy_weight = 0.1
loss_divisor = 16.0


def contract_rows(left, right):
    return lax.dot_general(
        left, right, (((0,), (0,)), ((), ())), preferred_element_type=jnp.float32
    )


def contract_cols(left, right):
    return lax.dot_general(
        left, right, (((1,), (1,)), ((), ())), preferred_element_type=jnp.float32
    )


def silu_slope(pre_value):
    sigma = jax.nn.sigmoid(pre_value)
    return sigma * (1.0 + pre_value * (1.0 - sigma))


def importance_trace_gradients(
    learner_output, acting_policy_logits, actions, rewards, episode_finished
):
    number_of_actions = acting_policy_logits.shape[-1]
    logits = learner_output[:, :, :number_of_actions]
    values = learner_output[:, :, number_of_actions]
    log_policy = jax.nn.log_softmax(logits[:, :-1], axis=-1)
    log_behave = jax.nn.log_softmax(acting_policy_logits, axis=-1)
    chosen = (
        actions[:, :, None] == jnp.arange(number_of_actions, dtype=jnp.int32)[None, None, :]
    ).astype(jnp.float32)
    ratio = jnp.exp(jnp.sum((log_policy - log_behave) * chosen, axis=-1))
    clipped = jnp.minimum(ratio, 1.0)
    discount = discount_rate * (1.0 - episode_finished.astype(jnp.float32))
    current = values[:, :-1]
    following = values[:, 1:]
    deltas = clipped * (rewards + discount * following - current)

    def backward_step(carried, step_item):
        delta_now, factor_now = step_item
        carried = delta_now + factor_now * carried
        return (carried, carried)

    start_carry = jnp.zeros((values.shape[0],), jnp.float32)
    _, corrections = lax.scan(
        backward_step, start_carry, (deltas.T, (discount * clipped).T), reverse=True
    )
    targets = current + corrections.T
    next_targets = jnp.concatenate([targets[:, 1:], values[:, -1:]], axis=1)
    advantage = clipped * (rewards + discount * next_targets - current)
    probability = jnp.exp(log_policy)
    entropy = -jnp.sum(probability * log_policy, axis=-1)
    logit_grad = (
        -advantage[..., None] * (chosen - probability)
        + entropy_weight * probability * (log_policy + entropy[..., None])
    ) / loss_divisor
    value_grad = -value_weight * (targets - current) / loss_divisor
    step_grad = jnp.concatenate([logit_grad, value_grad[..., None]], axis=-1)
    last_row = jnp.zeros((values.shape[0], 1, number_of_actions + 1), jnp.float32)
    return jnp.concatenate([step_grad, last_row], axis=1)


def per_device(
    observations,
    next_observations,
    trunk_weights,
    head_weights,
    acting_policy_logits,
    actions,
    rewards,
    episode_finished,
):
    traj_count, step_count, feature_block = observations.shape
    learner_rows = traj_count * step_count
    number_of_actions = acting_policy_logits.shape[-1]
    layer_total = trunk_weights.shape[0]
    own_rows = observations.reshape(learner_rows, feature_block)
    gathered_weights = [
        lax.all_gather(trunk_weights[layer_index], "dp", axis=0, tiled=True)
        for layer_index in range(layer_total)
    ]
    joined = jnp.concatenate([own_rows, next_observations], axis=0)
    inputs_full = []
    products_block = []
    current = joined
    for forward_layer_index in range(layer_total):
        forward_whole = lax.all_gather(current, "group", axis=1, tiled=True)
        inputs_full.append(forward_whole)
        product = jnp.dot(
            forward_whole, gathered_weights[forward_layer_index], preferred_element_type=jnp.float32
        )
        products_block.append(product)
        current = jax.nn.silu(product).astype(jnp.bfloat16)
    partial_head = jnp.dot(current, head_weights, preferred_element_type=jnp.float32)
    totals = lax.psum(partial_head, "group")
    inputs_full, products_block, last_block, totals = (inputs_full, products_block, current, totals)
    inputs_full = [whole[:learner_rows] for whole in inputs_full]
    products_block = [block[:learner_rows] for block in products_block]
    last_block = last_block[:learner_rows]
    head_out = totals[:learner_rows]
    actor_logits = totals[learner_rows:, :number_of_actions]
    learner_output = head_out.reshape(traj_count, step_count, number_of_actions + 1)
    output_gradient = importance_trace_gradients(
        learner_output, acting_policy_logits, actions, rewards, episode_finished
    )
    output_gradient = output_gradient.reshape(learner_rows, number_of_actions + 1).astype(
        jnp.bfloat16
    )
    head_partial = contract_rows(last_block, output_gradient)
    head_grads = lax.psum_scatter(head_partial, "dp", scatter_dimension=0, tiled=True)
    input_grad = contract_cols(output_gradient, head_weights)
    grad_list = [None] * layer_total
    for layer_index in range(layer_total - 1, -1, -1):
        pre_grad = (input_grad * silu_slope(products_block[layer_index])).astype(jnp.bfloat16)
        all_inputs = lax.all_to_all(
            inputs_full[layer_index], "dp", split_axis=1, concat_axis=0, tiled=True
        )
        all_upstream = lax.all_gather(pre_grad, "dp", axis=0, tiled=True)
        grad_list[layer_index] = contract_rows(all_inputs, all_upstream)
        if layer_index > 0:
            full_grad = contract_cols(pre_grad, gathered_weights[layer_index])
            input_grad = lax.psum_scatter(full_grad, "group", scatter_dimension=1, tiled=True)
    return (jnp.stack(grad_list), head_grads, actor_logits)


def solution(mesh):
    in_specs = (
        P("dp", None, "group"),
        P("dp", "group"),
        P(None, "dp", "group"),
        P("group", None),
        P("dp", None, None),
        P("dp", None),
        P("dp", None),
        P("dp", None),
    )
    out_specs = (P(None, "dp", "group"), P(("group", "dp"), None), P("dp", None))
    return jax.shard_map(
        per_device, mesh=mesh, in_specs=in_specs, out_specs=out_specs, check_vma=False
    )
```

profile of v0, /device:TPU:0, one launch (start us, length us, event | category | flops | bytes accessed | tf_op | source)
XLA Modules:
  0.0 727.3 jit_solution(5411754395285372085)
XLA Ops:
  7.2 0.0 copy-start
  7.2 0.0 all-gather.9.cloned.1.call-start
  7.2 2.6 pad_maximum_fusion.1
  9.8 0.0 all-gather.9.cloned.1.call-update
  9.9 0.0 all-gather.17.cloned.1.call-start
  9.9 1.5 fusion.27
  11.4 0.0 all-gather.17.cloned.1.call-update
  11.5 0.0 all-gather.19.cloned.1.call-start
  11.5 0.7 all-gather.19.cloned.1.call-update
  12.2 0.0 copy-start.5
  12.2 0.0 all-gather.11.cloned.1.call-start
  12.3 62.2 %all-gather.9.cloned.1.call-done = bf16[640,4096]{1,0:T(8,128)(2,1)} async-done(((bf16[640,1024]{1,0:T(8,128)(2,1)}), bf16[640,4096]{1,0:T(8,128)(2,1)}) %all-gather.9.cloned.1.call-update) | async-done | bytes 5242896 | tf_op jit(solution)/shard_map/all_gather | solution.py:95
  74.5 83.7 %all-gather.17.cloned.1.call-done = bf16[1,4096,1024]{2,1,0:T(8,128)(2,1)} async-done(((bf16[1,512,1024]{2,1,0:T(8,128)(2,1)}), bf16[1,4096,1024]{2,1,0:T(8,128)(2,1)}) %all-gather.17.cloned.1.call-update) | async-done | bytes 8388624 | tf_op jit(solution)/shard_map/all_gather | solution.py:87
  158.1 10.7 %multiply_convert_fusion.1 = (bf16[640,1024]{1,0:T(8,128)(2,1)}, f32[640,1024]{1,0:T(8,128)S(1)}) fusion(bf16[640,4096]{1,0:T(8,128)(2,1)} %all-gather.9.cloned.1.call-done, bf16[1,4096,1024]{2,1,0:T(8,128)(2,1)} %all-gather.17.cloned.1.call-done), kind=kOutput, calls=%fused_computation.12 | convolution fusion | flops 5371985920 | bytes 17563648 | tf_op jit(solution)/shard_map/dot_general | solution.py:97
  168.9 0.0 all-gather.11.cloned.1.call-update
  168.9 0.0 reduce-scatter.3.cloned.1.call-start
  169.0 0.0 copy-start.8
  169.0 0.0 copy-start.6
  169.0 0.0 copy-start.7
  169.1 71.2 %all-gather.19.cloned.1.call-done = bf16[1,4096,1024]{2,1,0:T(8,128)(2,1)} async-done(((bf16[1,512,1024]{2,1,0:T(8,128)(2,1)}), bf16[1,4096,1024]{2,1,0:T(8,128)(2,1)}) %all-gather.19.cloned.1.call-update) | async-done | bytes 8388624 | tf_op jit(solution)/shard_map/all_gather | solution.py:87
  240.3 62.1 %all-gather.11.cloned.1.call-done = bf16[640,4096]{1,0:T(8,128)(2,1)} async-done(((bf16[640,1024]{1,0:T(8,128)(2,1)}), bf16[640,4096]{1,0:T(8,128)(2,1)}) %all-gather.11.cloned.1.call-update) | async-done | bytes 5242896 | tf_op jit(solution)/shard_map/all_gather | solution.py:95
  302.4 10.9 %multiply_convert_fusion = (bf16[640,1024]{1,0:T(8,128)(2,1)S(1)}, f32[640,1024]{1,0:T(8,128)}) fusion(bf16[640,4096]{1,0:T(8,128)(2,1)} %all-gather.11.cloned.1.call-done, bf16[1,4096,1024]{2,1,0:T(8,128)(2,1)} %all-gather.19.cloned.1.call-done), kind=kOutput, calls=%fused_computation.11 | convolution fusion | flops 5371985920 | bytes 17563648 | tf_op jit(solution)/shard_map/dot_general | solution.py:97
  313.3 1.1 copy-done.3
  314.3 0.4 fusion.28
  314.8 16.2 %psum.7 = f32[640,19]{0,1:T(8,128)S(1)} all-reduce(f32[640,19]{0,1:T(8,128)S(1)} %fusion.28), channel_id=1, replica_groups=mesh['group'=4,'dp'=8] {'group'}, use_global_device_ids=true, to_apply=%region_0.1 | all-reduce | flops 12160 | bytes 97280 | tf_op jit(solution)/shard_map/psum | solution.py:103
  331.0 0.1 reshape.32
  331.2 0.1 slice.56
  331.3 0.1 multiply_bitcast_fusion
  331.3 0.1 copy.50
  331.4 0.1 copy.49
  331.5 4.7 while.17
  336.3 0.1 copy.51
  336.4 0.1 slice.55
  336.4 0.1 fusion.25
  336.6 0.1 convert_element_type.26
  336.7 3.4 multiply_convert_fusion.3
  340.1 11.5 %fusion.2 = f32[512,4096]{1,0:T(8,128)} fusion(bf16[512,1024]{1,0:T(8,128)(2,1)} %multiply_convert_fusion.3, bf16[1,4096,1024]{2,1,0:T(8,128)(2,1)} %all-gather.19.cloned.1.call-done), kind=kOutput, calls=%fused_computation.3 | convolution fusion | flops 4294967296 | bytes 17825792 | tf_op jit(solution)/shard_map/dot_general | solution.py:19
  351.7 0.0 reduce-scatter.3.cloned.1.call-update
  351.7 0.0 all-gather.15.cloned.1.call-start
  351.7 0.5 all-gather.15.cloned.1.call-update
  352.3 4.7 slice.62
  357.0 6.6 copy.47
  363.6 4.6 all-to-all-start
  368.2 0.2 all-gather.13.cloned.1.call-start
  368.4 69.6 %reduce-scatter.3.cloned.1.call-done = f32[512,1024]{1,0:T(8,128)} async-done(((f32[512,4096]{1,0:T(8,128)}), f32[512,1024]{1,0:T(8,128)}) %reduce-scatter.3.cloned.1.call-update) | async-done | bytes 2097168 | tf_op jit(solution)/shard_map/reduce_scatter | solution.py:130
  438.0 3.3 multiply_convert_fusion.2
  441.3 0.0 all-gather.13.cloned.1.call-update
  441.3 0.0 slice-start
  441.3 2.2 slice-done
  443.5 2.4 copy.55
  445.9 50.0 %all-to-all-done = bf16[512,8,512]{0,2,1:T(8,128)(2,1)} async-done(((bf16[512,8,512]{0,2,1:T(8,128)(2,1)}), bf16[512,8,512]{0,2,1:T(8,128)(2,1)}, u32[]{:S(2)}, u32[]{:S(2)}) %all-to-all-start) | async-done | bytes 4194336 | tf_op jit(solution)/shard_map/all_to_all | solution.py:123
  495.9 4.6 all-to-all-start.1
  500.5 0.0 reduce-scatter.5.cloned.1.call-start
  500.5 6.6 copy.48
  507.2 0.6 slice.70
  507.8 0.0 copy-done.4
  507.8 0.9 fusion.8
  508.7 0.0 reduce-scatter.5.cloned.1.call-update
  508.7 146.3 %all-to-all-done.1 = bf16[512,8,512]{2,0,1:T(8,128)(2,1)} async-done(((bf16[512,8,512]{2,0,1:T(8,128)(2,1)}), bf16[512,8,512]{2,0,1:T(8,128)(2,1)}, u32[]{:S(2)}, u32[]{:S(2)}) %all-to-all-start.1) | async-done | bytes 4194336 | tf_op jit(solution)/shard_map/all_to_all | solution.py:123
  655.0 8.3 %convolution_bitcast_fusion = f32[1,512,1024]{2,1,0:T(8,128)S(1)} fusion(bf16[4096,512]{1,0:T(8,128)(2,1)} %bitcast.13, bf16[4096,1024]{1,0:T(8,128)(2,1)} %all-gather.15.cloned.1.call-done), kind=kOutput, calls=%fused_computation.15 | convolution fusion | flops 4294967296 | bytes 14680064 | tf_op jit(solution)/shard_map/dot_general | solution.py:13
  663.3 26.0 %all-gather.13.cloned.1.call-done = bf16[4096,1024]{1,0:T(8,128)(2,1)} async-done(((bf16[512,1024]{1,0:T(8,128)(2,1)}), bf16[4096,1024]{1,0:T(8,128)(2,1)}) %all-gather.13.cloned.1.call-update) | async-done | bytes 8388624 | tf_op jit(solution)/shard_map/all_gather | solution.py:126
  689.3 8.2 %convolution_bitcast_fusion.1 = f32[1,512,1024]{2,1,0:T(8,128)S(1)} fusion(bf16[4096,512]{1,0:T(8,128)(2,1)} %bitcast.68, bf16[4096,1024]{1,0:T(8,128)(2,1)} %all-gather.13.cloned.1.call-done), kind=kOutput, calls=%fused_computation.16 | convolution fusion | flops 4294967296 | bytes 14680064 | tf_op jit(solution)/shard_map/dot_general | solution.py:13
  697.5 2.5 pad_maximum_fusion
  700.0 20.5 %reduce-scatter.5.cloned.1.call-done = f32[128,19]{0,1:T(8,128)} async-done(((f32[1024,19]{0,1:T(8,128)}), f32[128,19]{0,1:T(8,128)}) %reduce-scatter.5.cloned.1.call-update) | async-done | bytes 9744 | tf_op jit(solution)/shard_map/reduce_scatter | solution.py:118
  (153 shorter events, 3.9 us)
Async XLA Ops:
  7.2 307.2 %copy-start = (bf16[1024,19]{0,1:T(8,128)(2,1)S(1)}, bf16[1024,19]{0,1:T(8,128)(2,1)}, u32[]{:S(2)}) copy-start(bf16[1024,19]{0,1:T(8,128)(2,1)} %param.14) | copy-start | bytes 116740
  7.2 2.7 copy-start.2
  7.2 67.3 %all-gather.9.cloned.1.call-start = ((), (), s32[]{:S(2)}) async-start(), calls=%async_computation.4 | async-start | bytes 6553600 | tf_op jit(solution)/shard_map/all_gather | solution.py:95
  9.9 148.3 %all-gather.17.cloned.1.call-start = ((), (), s32[]{:S(2)}) async-start(), calls=%async_computation.10 | async-start | bytes 9437184 | tf_op jit(solution)/shard_map/all_gather | solution.py:87
  11.5 228.8 %all-gather.19.cloned.1.call-start = ((), (), s32[]{:S(2)}) async-start(), calls=%async_computation.11 | async-start | bytes 9437184 | tf_op jit(solution)/shard_map/all_gather | solution.py:87
  12.2 156.8 %copy-start.5 = (f32[8,63,18]{1,0,2:T(8,128)S(1)}, f32[8,63,18]{1,0,2:T(8,128)}, u32[]{:S(2)}) copy-start(f32[8,63,18]{1,0,2:T(8,128)} %param.15) | copy-start | bytes 108868
  12.2 290.2 %all-gather.11.cloned.1.call-start = ((), (), s32[]{:S(2)}) async-start(), calls=%async_computation.5 | async-start | bytes 6553600 | tf_op jit(solution)/shard_map/all_gather | solution.py:95
  168.9 269.1 %reduce-scatter.3.cloned.1.call-start = ((), (), s32[]{:S(2)}) async-start(), calls=%async_computation.6 | async-start | bytes 10485760 | tf_op jit(solution)/shard_map/reduce_scatter | solution.py:130
  169.0 162.1 %copy-start.8 = (s32[8,63]{1,0:T(8,128)S(1)}, s32[8,63]{1,0:T(8,128)}, u32[]{:S(2)}) copy-start(s32[8,63]{1,0:T(8,128)} %param.16) | copy-start | bytes 6052
  169.0 162.2 %copy-start.6 = (s32[8,63]{1,0:T(8,128)S(1)}, s32[8,63]{1,0:T(8,128)}, u32[]{:S(2)}) copy-start(s32[8,63]{1,0:T(8,128)} %param.18) | copy-start | bytes 6052
  169.0 162.2 %copy-start.7 = (f32[8,63]{1,0:T(8,128)S(1)}, f32[8,63]{1,0:T(8,128)}, u32[]{:S(2)}) copy-start(f32[8,63]{1,0:T(8,128)} %param.17) | copy-start | bytes 6052
  313.3 1.1 copy-start.3
  351.7 303.3 %all-gather.15.cloned.1.call-start = ((), (), s32[]{:S(2)}) async-start(), calls=%async_computation.8 | async-start | bytes 9437184 | tf_op jit(solution)/shard_map/all_gather | solution.py:126
  363.6 132.3 %all-to-all-start = ((bf16[512,8,512]{0,2,1:T(8,128)(2,1)}), bf16[512,8,512]{0,2,1:T(8,128)(2,1)}, u32[]{:S(2)}, u32[]{:S(2)}) async-start(bf16[512,8,512]{0,2,1:T(8,128)(2,1)} %bitcast.65), calls=%async_computation | async-start | bytes 8388608 | tf_op jit(solution)/shard_map/all_to_all | solution.py:123
  368.2 321.1 %all-gather.13.cloned.1.call-start = ((), (), s32[]{:S(2)}) async-start(), calls=%async_computation.7 | async-start | bytes 9437184 | tf_op jit(solution)/shard_map/all_gather | solution.py:126
  441.3 2.2 slice-start
  495.9 159.1 %all-to-all-start.1 = ((bf16[512,8,512]{2,0,1:T(8,128)(2,1)}), bf16[512,8,512]{2,0,1:T(8,128)(2,1)}, u32[]{:S(2)}, u32[]{:S(2)}) async-start(bf16[512,8,512]{2,0,1:T(8,128)(2,1)} %bitcast.66), calls=%async_computation.2 | async-start | bytes 8388608 | tf_op jit(solution)/shard_map/all_to_all | solution.py:123
  500.5 220.0 %reduce-scatter.5.cloned.1.call-start = ((), (), s32[]{:S(2)}) async-start(), calls=%async_computation.9 | async-start | bytes 110592 | tf_op jit(solution)/shard_map/reduce_scatter | solution.py:118
  500.5 7.3 copy-start.4
  689.3 31.2 %copy-start.1 = (bf16[1024,19]{0,1:T(8,128)(2,1)S(1)}, bf16[1024,19]{0,1:T(8,128)(2,1)}, u32[]{:S(2)}) copy-start(bf16[1024,19]{0,1:T(8,128)(2,1)} %param.14) | copy-start | bytes 116740
Sparse Core Ops, SparseCore 0:
  10.4 64.0 all-gather.8
  76.1 82.0 all-gather.16
  159.7 80.5 all-gather.18
  242.6 59.7 all-gather.10
  351.8 86.1 reduce-scatter.2
  439.4 153.6 all-gather.14
  594.7 94.5 all-gather.12
  692.1 28.3 reduce-scatter.4
where the time goes:
time: 728 us; the launch traced here: 727 us
  waiting for transfers between devices  593 us (81%)
  matrix products  54.4 us (7%)
  local copies, waits for them, and re-layouts  28.9 us (4%)
  blocking collectives  16.2 us (2%)
  between operations  14.3 us (2%)
  other arithmetic  9.97 us (1%)
  starting transfers between devices  9.68 us (1%)
    all_to_all x2, waiting for transfers between devices, per_device(): lax.all_to_all(inputs_full[layer_index], 'dp', split_axis=1, concat_axis=...  196 us
    all_gather x2, waiting for transfers between devices, per_device(): lax.all_gather(trunk_weights[layer_index], 'dp', axis=0, tiled=True)  155 us
    all_gather x2, waiting for transfers between devices, per_device(): forward_whole = lax.all_gather(current, 'group', axis=1, tiled=True)  124 us
    reduce_scatter x1, waiting for transfers between devices, per_device(): lax.psum_scatter(full_grad, 'group', scatter_dimension=1, tiled=True)  69.6 us
    all_gather x2, waiting for transfers between devices, per_device(): all_upstream = lax.all_gather(pre_grad, 'dp', axis=0, tiled=True)  26 us
    dot_general x2, matrix products, per_device(): jnp.dot(forward_whole, gathered_weights[forward_layer_index], preferred_e...  21.6 us
    reduce_scatter x1, waiting for transfers between devices, per_device(): lax.psum_scatter(head_partial, 'dp', scatter_dimension=0, tiled=True)  20.5 us
    dot_general x3, matrix products, contract_rows(): lax.dot_general(left, right, (((0,), (0,)), ((), ())), preferred_element_...  17.4 us
  transfers between devices with their start and end apart: 10, of which 9 were waited for; matrix products, arithmetic and copies ran while one was open for 8% of the time, Pallas kernels for 0%

commit v1 on v0

--- a/solution.py
+++ b/solution.py
@@ -92,7 +92,14 @@
     products_block = []
     current = joined
     for forward_layer_index in range(layer_total):
-        forward_whole = lax.all_gather(current, "group", axis=1, tiled=True)
+        ring = [current]
+        for hop in range(3):
+            ring.append(lax.ppermute(ring[-1], "group", [(dev, (dev + 1) % 4) for dev in range(4)]))
+        forward_whole = jnp.roll(
+            jnp.concatenate(ring[::-1], axis=1),
+            (lax.axis_index("group") + 1) * ring[0].shape[1],
+            axis=1,
+        )
         inputs_full.append(forward_whole)
         product = jnp.dot(
             forward_whole, gathered_weights[forward_layer_index], preferred_element_type=jnp.float32

time: 728 us -> 683 us (0.938)
  waiting for transfers between devices: 593 us -> 490 us
  other arithmetic: 9.97 us -> 62.3 us
    ppermute x0 -> x6, waiting for transfers between devices: none -> 177 us  [per_device(): lax.ppermute(ring[-1], 'group', [(dev, (dev + 1) % 4) for dev in range(4)])]
    all_gather x2, waiting for transfers between devices: 155 us -> 0.02 us  [per_device(): lax.all_gather(trunk_weights[layer_index], 'dp', axis=0, tiled=True)]
    all_gather x2 -> x0, waiting for transfers between devices: 124 us -> none  [per_device(): forward_whole = lax.all_gather(current, 'group', axis=1, tiled=True)]
    concatenate x0 -> x2, other arithmetic: none -> 54.8 us  [per_device(): jnp.roll(jnp.concatenate(ring[::-1], axis=1), (lax.axis_index('group') +...]
  transfers between devices with their start and end apart: 10 -> 14, of which waited for: 9 -> 11; matrix products, arithmetic and copies ran while one was open for 8% -> 16% of each run, Pallas kernels for 0% -> 0%
where the time goes in v1:
time: 683 us
  waiting for transfers between devices  490 us (72%)
  other arithmetic  62.3 us (9%)
  matrix products  53.9 us (8%)
  local copies, waits for them, and re-layouts  32.4 us (5%)
  blocking collectives  14.8 us (2%)
  between operations  14.3 us (2%)
  starting transfers between devices  13.2 us (2%)
    all_to_all x2, waiting for transfers between devices, per_device(): lax.all_to_all(inputs_full[layer_index], 'dp', split_axis=1, concat_axis=...  196 us
    ppermute x6, waiting for transfers between devices, per_device(): lax.ppermute(ring[-1], 'group', [(dev, (dev + 1) % 4) for dev in range(4)])  177 us
    reduce_scatter x1, waiting for transfers between devices, per_device(): lax.psum_scatter(full_grad, 'group', scatter_dimension=1, tiled=True)  70 us
    concatenate x2, other arithmetic, per_device(): jnp.roll(jnp.concatenate(ring[::-1], axis=1), (lax.axis_index('group') +...  54.8 us
    all_gather x2, waiting for transfers between devices, per_device(): all_upstream = lax.all_gather(pre_grad, 'dp', axis=0, tiled=True)  25.6 us
    dot_general x2, matrix products, per_device(): jnp.dot(forward_whole, gathered_weights[forward_layer_index], preferred_e...  21 us
    reduce_scatter x1, waiting for transfers between devices, per_device(): lax.psum_scatter(head_partial, 'dp', scatter_dimension=0, tiled=True)  20.7 us
    dot_general x3, matrix products, contract_rows(): lax.dot_general(left, right, (((0,), (0,)), ((), ())), preferred_element_...  17.4 us
  transfers between devices with their start and end apart: 14, of which 11 were waited for; matrix products, arithmetic and copies ran while one was open for 16% of the time, Pallas kernels for 0%

profile of v1, /device:TPU:0, one launch (start us, length us, event | category | flops | bytes accessed | tf_op | source)
XLA Modules:
  0.0 682.5 jit_solution(9371545643709056528)
XLA Ops:
  7.2 0.0 copy-start
  7.2 0.0 all-gather.11.cloned.1.call-start
  7.2 3.1 fusion.43
  10.4 0.0 all-gather.11.cloned.1.call-update
  10.4 0.0 all-gather.13.cloned.1.call-start
  10.4 0.7 all-gather.13.cloned.1.call-update
  11.1 0.0 reduce-scatter.3.cloned.1.call-start
  11.2 0.1 pad_maximum_fusion.1
  11.3 3.0 collective-permute-start
  14.3 29.7 %collective-permute-done = bf16[640,1024]{1,0:T(8,128)(2,1)S(1)} collective-permute-done((bf16[640,1024]{1,0:T(8,128)(2,1)S(1)}, bf16[640,1024]{1,0:T(8,128)(2,1)S(1)}, u32[]{:S(2)}, u32[]{:S(2)}) %collective-permute-start) | collective-permute-done | bytes 1310752 | tf_op jit(solution)/shard_map/ppermute | solution.py:97
  44.1 0.8 collective-permute-start.1
  44.9 30.3 %collective-permute-done.1 = bf16[640,1024]{1,0:T(8,128)(2,1)} collective-permute-done((bf16[640,1024]{1,0:T(8,128)(2,1)S(1)}, bf16[640,1024]{1,0:T(8,128)(2,1)}, u32[]{:S(2)}, u32[]{:S(2)}) %collective-permute-start.1) | collective-permute-done | bytes 1310752 | tf_op jit(solution)/shard_map/ppermute | solution.py:97
  75.1 30.4 %collective-permute-done.2 = bf16[640,1024]{1,0:T(8,128)(2,1)} collective-permute-done((bf16[640,1024]{1,0:T(8,128)(2,1)}, bf16[640,1024]{1,0:T(8,128)(2,1)}, u32[]{:S(2)}, u32[]{:S(2)}) %collective-permute-start.2) | collective-permute-done | bytes 1310752 | tf_op jit(solution)/shard_map/ppermute | solution.py:97
  105.5 44.2 %fusion.18 = bf16[640,4096]{1,0:T(8,128)(2,1)} fusion(s32[]{:T(128)S(6)} %select_n.13, bf16[640,1024]{1,0:T(8,128)(2,1)} %collective-permute-done.2, bf16[640,1024]{1,0:T(8,128)(2,1)} %collective-permute-done.1, bf16[640,1024]{1,0:T(8,128)(2,1)S(1)} %collective-permute-done, bf16[512,1024]{1,0:T(8,128)(2,1)S(1)} %bitcast.70, bf16[128,1024]{1,0:T(8,128)(2,1)S(1)} %copy-done.7), kind=kLoop, calls=%fused_computation.37 | loop fusion | flops 52428800 | bytes 10485764 | tf_op jit(solution)/shard_map/jit(_roll_dynamic)/concatenate | solution.py:98
  149.7 10.1 %multiply_convert_fusion.1 = (bf16[640,1024]{1,0:T(8,128)(2,1)S(1)}, f32[640,1024]{1,0:T(8,128)S(1)}) fusion(bf16[640,4096]{1,0:T(8,128)(2,1)} %fusion.18, bf16[1,4096,1024]{2,1,0:T(8,128)(2,1)} %all-gather.11.cloned.1.call-done), kind=kOutput, calls=%fused_computation.46 | convolution fusion | flops 5371985920 | bytes 17563648 | tf_op jit(solution)/shard_map/dot_general | solution.py:104
  159.9 1.1 copy-done.5
  161.0 29.4 %collective-permute-done.3 = bf16[640,1024]{1,0:T(8,128)(2,1)S(1)} collective-permute-done((bf16[640,1024]{1,0:T(8,128)(2,1)S(1)}, bf16[640,1024]{1,0:T(8,128)(2,1)S(1)}, u32[]{:S(2)}, u32[]{:S(2)}) %collective-permute-start.3) | collective-permute-done | bytes 1310752 | tf_op jit(solution)/shard_map/ppermute | solution.py:97
  190.4 1.1 copy-done.6
  191.5 28.7 %collective-permute-done.4 = bf16[640,1024]{1,0:T(8,128)(2,1)} collective-permute-done((bf16[640,1024]{1,0:T(8,128)(2,1)S(1)}, bf16[640,1024]{1,0:T(8,128)(2,1)}, u32[]{:S(2)}, u32[]{:S(2)}) %collective-permute-start.4) | collective-permute-done | bytes 1310752 | tf_op jit(solution)/shard_map/ppermute | solution.py:97
  220.3 28.0 %collective-permute-done.5 = bf16[640,1024]{1,0:T(8,128)(2,1)} collective-permute-done((bf16[640,1024]{1,0:T(8,128)(2,1)}, bf16[640,1024]{1,0:T(8,128)(2,1)}, u32[]{:S(2)}, u32[]{:S(2)}) %collective-permute-start.5) | collective-permute-done | bytes 1310752 | tf_op jit(solution)/shard_map/ppermute | solution.py:97
  248.2 10.6 %fusion.11 = bf16[640,4096]{1,0:T(8,128)(2,1)} fusion(s32[]{:T(128)S(6)} %select_n.13, bf16[640,1024]{1,0:T(8,128)(2,1)} %collective-permute-done.5, bf16[640,1024]{1,0:T(8,128)(2,1)} %collective-permute-done.4, bf16[640,1024]{1,0:T(8,128)(2,1)} %copy-done.6, bf16[640,1024]{1,0:T(8,128)(2,1)} %copy-done.5), kind=kLoop, calls=%fused_computation.30 | loop fusion | flops 41943040 | bytes 10485764 | tf_op jit(solution)/shard_map/jit(_roll_dynamic)/concatenate | solution.py:98
  258.9 0.0 copy-start.10
  258.9 0.0 all-gather.13.cloned.1.call-done
  258.9 10.9 %multiply_convert_fusion = (bf16[640,1024]{1,0:T(8,128)(2,1)S(1)}, f32[640,1024]{1,0:T(8,128)}) fusion(bf16[640,4096]{1,0:T(8,128)(2,1)} %fusion.11, bf16[1,4096,1024]{2,1,0:T(8,128)(2,1)} %all-gather.13.cloned.1.call-done), kind=kOutput, calls=%fused_computation.45 | convolution fusion | flops 5371985920 | bytes 17563648 | tf_op jit(solution)/shard_map/dot_general | solution.py:104
  269.8 1.1 copy-done.3
  270.9 0.4 fusion.44
  271.3 14.8 %psum.7 = f32[640,19]{0,1:T(8,128)S(1)} all-reduce(f32[640,19]{0,1:T(8,128)S(1)} %fusion.44), channel_id=1, replica_groups=mesh['group'=4,'dp'=8] {'group'}, use_global_device_ids=true, to_apply=%region_0.2 | all-reduce | flops 12160 | bytes 97280 | tf_op jit(solution)/shard_map/psum | solution.py:110
  286.1 0.1 reshape.32
  286.4 0.1 slice.56
  286.4 0.1 multiply_bitcast_fusion
  286.5 0.1 copy.50
  286.6 0.1 copy.49
  286.7 4.7 while.17
  291.4 0.1 copy.51
  291.5 0.1 slice.55
  291.6 0.1 fusion.41
  291.8 0.1 convert_element_type.26
  291.9 3.5 multiply_convert_fusion.3
  295.3 11.5 %fusion.2 = f32[512,4096]{1,0:T(8,128)} fusion(bf16[512,1024]{1,0:T(8,128)(2,1)} %multiply_convert_fusion.3, bf16[1,4096,1024]{2,1,0:T(8,128)(2,1)} %all-gather.13.cloned.1.call-done), kind=kOutput, calls=%fused_computation.21 | convolution fusion | flops 4294967296 | bytes 17825792 | tf_op jit(solution)/shard_map/dot_general | solution.py:19
  306.8 0.0 reduce-scatter.3.cloned.1.call-update
  306.9 0.0 all-gather.9.cloned.1.call-start
  306.9 0.5 all-gather.9.cloned.1.call-update
  307.4 4.7 slice.62
  312.1 6.6 copy.47
  318.7 4.6 all-to-all-start
  323.3 0.0 all-gather.7.cloned.1.call-start
  323.3 70.0 %reduce-scatter.3.cloned.1.call-done = f32[512,1024]{1,0:T(8,128)} async-done(((f32[512,4096]{1,0:T(8,128)}), f32[512,1024]{1,0:T(8,128)}) %reduce-scatter.3.cloned.1.call-update) | async-done | bytes 2097168 | tf_op jit(solution)/shard_map/reduce_scatter | solution.py:137
  393.3 3.4 multiply_convert_fusion.2
  396.7 0.0 all-gather.7.cloned.1.call-update
  396.7 2.2 slice-done
  398.9 2.4 copy.55
  401.3 49.2 %all-to-all-done = bf16[512,8,512]{0,2,1:T(8,128)(2,1)} async-done(((bf16[512,8,512]{0,2,1:T(8,128)(2,1)}), bf16[512,8,512]{0,2,1:T(8,128)(2,1)}, u32[]{:S(2)}, u32[]{:S(2)}) %all-to-all-start) | async-done | bytes 4194336 | tf_op jit(solution)/shard_map/all_to_all | solution.py:130
  450.5 4.6 all-to-all-start.1
  455.1 0.0 reduce-scatter.5.cloned.1.call-start
  455.2 6.5 copy.48
  461.7 0.6 slice.70
  462.3 0.9 fusion.24
  463.2 0.0 reduce-scatter.5.cloned.1.call-update
  463.2 147.1 %all-to-all-done.1 = bf16[512,8,512]{2,0,1:T(8,128)(2,1)} async-done(((bf16[512,8,512]{2,0,1:T(8,128)(2,1)}), bf16[512,8,512]{2,0,1:T(8,128)(2,1)}, u32[]{:S(2)}, u32[]{:S(2)}) %all-to-all-start.1) | async-done | bytes 4194336 | tf_op jit(solution)/shard_map/all_to_all | solution.py:130
  610.3 8.3 %convolution_bitcast_fusion = f32[1,512,1024]{2,1,0:T(8,128)S(1)} fusion(bf16[4096,512]{1,0:T(8,128)(2,1)} %bitcast.13, bf16[4096,1024]{1,0:T(8,128)(2,1)} %all-gather.9.cloned.1.call-done), kind=kOutput, calls=%fused_computation.49 | convolution fusion | flops 4294967296 | bytes 14680064 | tf_op jit(solution)/shard_map/dot_general | solution.py:13
  618.7 25.6 %all-gather.7.cloned.1.call-done = bf16[4096,1024]{1,0:T(8,128)(2,1)} async-done(((bf16[512,1024]{1,0:T(8,128)(2,1)}), bf16[4096,1024]{1,0:T(8,128)(2,1)}) %all-gather.7.cloned.1.call-update) | async-done | bytes 8388624 | tf_op jit(solution)/shard_map/all_gather | solution.py:133
  644.3 8.2 %convolution_bitcast_fusion.1 = f32[1,512,1024]{2,1,0:T(8,128)S(1)} fusion(bf16[4096,512]{1,0:T(8,128)(2,1)} %bitcast.68, bf16[4096,1024]{1,0:T(8,128)(2,1)} %all-gather.7.cloned.1.call-done), kind=kOutput, calls=%fused_computation.50 | convolution fusion | flops 4294967296 | bytes 14680064 | tf_op jit(solution)/shard_map/dot_general | solution.py:13
  652.5 2.5 pad_maximum_fusion
  655.0 20.7 %reduce-scatter.5.cloned.1.call-done = f32[128,19]{0,1:T(8,128)} async-done(((f32[1024,19]{0,1:T(8,128)}), f32[128,19]{0,1:T(8,128)}) %reduce-scatter.5.cloned.1.call-update) | async-done | bytes 9744 | tf_op jit(solution)/shard_map/reduce_scatter | solution.py:125
  (167 shorter events, 4.0 us)
Async XLA Ops:
  7.2 263.7 %copy-start = (bf16[1024,19]{0,1:T(8,128)(2,1)S(1)}, bf16[1024,19]{0,1:T(8,128)(2,1)}, u32[]{:S(2)}) copy-start(bf16[1024,19]{0,1:T(8,128)(2,1)} %param.16) | copy-start | bytes 116740
  7.2 4.0 copy-start.7
  7.2 4.0 copy-start.2
  7.2 142.5 %all-gather.11.cloned.1.call-start = ((), (), s32[]{:S(2)}) async-start(), calls=%async_computation.8 | async-start | bytes 9437184 | tf_op jit(solution)/shard_map/all_gather | solution.py:87
  10.4 248.5 %all-gather.13.cloned.1.call-start = ((), (), s32[]{:S(2)}) async-start(), calls=%async_computation.9 | async-start | bytes 9437184 | tf_op jit(solution)/shard_map/all_gather | solution.py:87
  11.1 382.2 %reduce-scatter.3.cloned.1.call-start = ((), (), s32[]{:S(2)}) async-start(), calls=%async_computation.4 | async-start | bytes 10485760 | tf_op jit(solution)/shard_map/reduce_scatter | solution.py:137
  11.3 32.8 %collective-permute-start = (bf16[640,1024]{1,0:T(8,128)(2,1)S(1)}, bf16[640,1024]{1,0:T(8,128)(2,1)S(1)}, u32[]{:S(2)}, u32[]{:S(2)}) collective-permute-start(bf16[640,1024]{1,0:T(8,128)(2,1)S(1)} %pad_maximum_fusion.1), channel_id=1, source_target_pairs={{0,8},{8,16},{16,24},{24,0},{1,9},{9,17},{17,25},{25,1},{2,10},{10... | collective-permute-start | bytes 3932168 | tf_op jit(solution)/shard_map/ppermute | solution.py:97
  44.1 31.1 %collective-permute-start.1 = (bf16[640,1024]{1,0:T(8,128)(2,1)S(1)}, bf16[640,1024]{1,0:T(8,128)(2,1)}, u32[]{:S(2)}, u32[]{:S(2)}) collective-permute-start(bf16[640,1024]{1,0:T(8,128)(2,1)S(1)} %collective-permute-done), channel_id=1, source_target_pairs={{0,8},{8,16},{16,24},{24,0},{1,9},{9,17},{17,25},{25,1},{2,10},{10... | collective-permute-start | bytes 3932168 | tf_op jit(solution)/shard_map/ppermute | solution.py:97
  75.1 30.4 %collective-permute-start.2 = (bf16[640,1024]{1,0:T(8,128)(2,1)}, bf16[640,1024]{1,0:T(8,128)(2,1)}, u32[]{:S(2)}, u32[]{:S(2)}) collective-permute-start(bf16[640,1024]{1,0:T(8,128)(2,1)} %collective-permute-done.1), channel_id=1, source_target_pairs={{0,8},{8,16},{16,24},{24,0},{1,9},{9,17},{17,25},{25,1},{2,10},{10... | collective-permute-start | bytes 3932168 | tf_op jit(solution)/shard_map/ppermute | solution.py:97
  149.7 70.5 %copy-start.8 = (f32[8,63,18]{1,0,2:T(8,128)S(1)}, f32[8,63,18]{1,0,2:T(8,128)}, u32[]{:S(2)}) copy-start(f32[8,63,18]{1,0,2:T(8,128)} %param.17) | copy-start | bytes 108868
  159.9 1.1 copy-start.5
  161.0 29.4 %collective-permute-start.3 = (bf16[640,1024]{1,0:T(8,128)(2,1)S(1)}, bf16[640,1024]{1,0:T(8,128)(2,1)S(1)}, u32[]{:S(2)}, u32[]{:S(2)}) collective-permute-start(bf16[640,1024]{1,0:T(8,128)(2,1)S(1)} %get-tuple-element.150), channel_id=1, source_target_pairs={{0,8},{8,16},{16,24},{24,0},{1,9},{9,17},{17,25},{25,1},{2,10},{10... | collective-permute-start | bytes 3932168 | tf_op jit(solution)/shard_map/ppermute | solution.py:97
  190.4 1.1 copy-start.6
  191.5 28.7 %collective-permute-start.4 = (bf16[640,1024]{1,0:T(8,128)(2,1)S(1)}, bf16[640,1024]{1,0:T(8,128)(2,1)}, u32[]{:S(2)}, u32[]{:S(2)}) collective-permute-start(bf16[640,1024]{1,0:T(8,128)(2,1)S(1)} %collective-permute-done.3), channel_id=1, source_target_pairs={{0,8},{8,16},{16,24},{24,0},{1,9},{9,17},{17,25},{25,1},{2,10},{10... | collective-permute-start | bytes 3932168 | tf_op jit(solution)/shard_map/ppermute | solution.py:97
  220.2 28.0 %collective-permute-start.5 = (bf16[640,1024]{1,0:T(8,128)(2,1)}, bf16[640,1024]{1,0:T(8,128)(2,1)}, u32[]{:S(2)}, u32[]{:S(2)}) collective-permute-start(bf16[640,1024]{1,0:T(8,128)(2,1)} %collective-permute-done.4), channel_id=1, source_target_pairs={{0,8},{8,16},{16,24},{24,0},{1,9},{9,17},{17,25},{25,1},{2,10},{10... | collective-permute-start | bytes 3932168 | tf_op jit(solution)/shard_map/ppermute | solution.py:97
  258.9 27.4 %copy-start.11 = (s32[8,63]{1,0:T(8,128)S(1)}, s32[8,63]{1,0:T(8,128)}, u32[]{:S(2)}) copy-start(s32[8,63]{1,0:T(8,128)} %param.18) | copy-start | bytes 6052
  258.9 27.6 %copy-start.9 = (s32[8,63]{1,0:T(8,128)S(1)}, s32[8,63]{1,0:T(8,128)}, u32[]{:S(2)}) copy-start(s32[8,63]{1,0:T(8,128)} %param.20) | copy-start | bytes 6052
  258.9 27.6 %copy-start.10 = (f32[8,63]{1,0:T(8,128)S(1)}, f32[8,63]{1,0:T(8,128)}, u32[]{:S(2)}) copy-start(f32[8,63]{1,0:T(8,128)} %param.19) | copy-start | bytes 6052
  269.8 1.1 copy-start.3
  306.9 303.5 %all-gather.9.cloned.1.call-start = ((), (), s32[]{:S(2)}) async-start(), calls=%async_computation.6 | async-start | bytes 9437184 | tf_op jit(solution)/shard_map/all_gather | solution.py:133
  318.7 131.8 %all-to-all-start = ((bf16[512,8,512]{0,2,1:T(8,128)(2,1)}), bf16[512,8,512]{0,2,1:T(8,128)(2,1)}, u32[]{:S(2)}, u32[]{:S(2)}) async-start(bf16[512,8,512]{0,2,1:T(8,128)(2,1)} %bitcast.66), calls=%async_computation | async-start | bytes 8388608 | tf_op jit(solution)/shard_map/all_to_all | solution.py:130
  323.3 321.0 %all-gather.7.cloned.1.call-start = ((), (), s32[]{:S(2)}) async-start(), calls=%async_computation.5 | async-start | bytes 9437184 | tf_op jit(solution)/shard_map/all_gather | solution.py:133
  396.7 2.2 slice-start
  450.5 159.8 %all-to-all-start.1 = ((bf16[512,8,512]{2,0,1:T(8,128)(2,1)}), bf16[512,8,512]{2,0,1:T(8,128)(2,1)}, u32[]{:S(2)}, u32[]{:S(2)}) async-start(bf16[512,8,512]{2,0,1:T(8,128)(2,1)} %bitcast.67), calls=%async_computation.2 | async-start | bytes 8388608 | tf_op jit(solution)/shard_map/all_to_all | solution.py:130
  455.1 7.2 %copy-start.4 = (bf16[640,1024]{1,0:T(8,128)(2,1)S(1)}, bf16[640,1024]{1,0:T(8,128)(2,1)}, u32[]{:S(2)}) copy-start(bf16[640,1024]{1,0:T(8,128)(2,1)} %copy-done.3) | copy-start | bytes 3932164
  455.1 220.6 %reduce-scatter.5.cloned.1.call-start = ((), (), s32[]{:S(2)}) async-start(), calls=%async_computation.7 | async-start | bytes 110592 | tf_op jit(solution)/shard_map/reduce_scatter | solution.py:125
  644.3 31.4 %copy-start.1 = (bf16[1024,19]{0,1:T(8,128)(2,1)S(1)}, bf16[1024,19]{0,1:T(8,128)(2,1)}, u32[]{:S(2)}) copy-start(bf16[1024,19]{0,1:T(8,128)(2,1)} %param.16) | copy-start | bytes 116740
Sparse Core Ops, SparseCore 0:
  10.5 84.7 all-gather.10
  96.9 80.5 all-gather.12
  307.0 86.2 reduce-scatter.2
  394.8 153.5 all-gather.8
  549.8 94.4 all-gather.6
  647.0 28.6 reduce-scatter.4
